TPU v7x, 32 devices: a whole 2x2x4 slice. The times are simulated.
32 devices in a mesh: seq: 4 (over y, core), head: 8 (over z, x).
Axes of the slice: x: 2, y: 2, z: 4, core: 2. Of those that a mesh axis runs over, the one named last changes fastest.
Arguments:
- queries: bfloat16 [8, 2048, 256], P('head', 'seq'), may hold values from -6 to 6
- keys: bfloat16 [1, 2048, 256], P(None, 'seq'), may hold values from -6 to 6
- values: bfloat16 [1, 2048, 256], P(None, 'seq'), may hold values from -6 to 6
- d_out: bfloat16 [8, 2048, 256], P('head', 'seq'), may hold values from -12 to 12
- doc_lengths: int32 [1, 8], replicated, may hold values from 1 to 768, 2048 in all within a row
- fold_order: int32 [8], replicated, may hold values from 0 to 7, each once
Outputs:
- grad_queries: bfloat16 [8, 2048, 256], P('head', 'seq')
- grad_keys: float32 [1, 2048, 256], P(None, ('seq', 'head'))
- grad_values: float32 [1, 2048, 256], P(None, ('seq', 'head'))
Inputs may be any that keep to these rules, and one draw needn't show every extreme that they name: `doc_lengths`: each row's 8 lengths are at least 1, sum to 2048, and the longest is exactly 768. fold_order names each of 0 to 7 once.
All inputs are finite; a program needn't handle non-finite values.
Results may differ from a plain program's by a relative error of at most 0.029.
Values may be sent and summed in bfloat16 or wider, within the bound.
A program may use at most 64 MiB of HBM per device.

v0:
```python
import functools

import jax
import jax.numpy as jnp
from jax import lax
from jax.experimental import pallas as pl
from jax.experimental.pallas import tpu as pltpu
from jax.sharding import PartitionSpec as P

HEAD_COUNT = 8


masked_value = -1e30


def contract_last(left, right):
    return lax.dot_general(
        left, right, (((1,), (1,)), ((), ())), preferred_element_type=jnp.float32
    )


def contract_first(left, right):
    return lax.dot_general(
        left, right, (((0,), (0,)), ((), ())), preferred_element_type=jnp.float32
    )


def block_grads(query_rows, grad_out, log_norm, grad_dot, key_part, value_part, allowed, scaling):
    scores = contract_last(query_rows, key_part) * scaling
    weights = jnp.exp(jnp.where(allowed, scores - log_norm, masked_value))
    weights_low = weights.astype(jnp.bfloat16)
    grad_prob = contract_last(grad_out, value_part)
    grad_score = (weights * (grad_prob - grad_dot)).astype(jnp.bfloat16)
    part_query = jnp.dot(grad_score, key_part, preferred_element_type=jnp.float32) * scaling
    part_key = contract_first(grad_score, query_rows) * scaling
    part_value = contract_first(weights_low, grad_out)
    return (part_query, part_key, part_value)


def owner_blocks(key_part, value_part, row_count):
    head_total = lax.axis_size("head")
    piece_len = key_part.shape[0] // head_total
    width = key_part.shape[1]
    moved = (
        lax.all_to_all(
            key_part.astype(jnp.bfloat16), "head", split_axis=0, concat_axis=0, tiled=True
        ).astype(key_part.dtype),
        lax.all_to_all(
            value_part.astype(jnp.bfloat16), "head", split_axis=0, concat_axis=0, tiled=True
        ).astype(value_part.dtype),
    )
    return tuple(
        (
            jnp.sum(item.reshape(row_count, head_total // row_count, piece_len, width), axis=1)
            for item in moved
        )
    )


def per_device(queries, keys, values, d_out, doc_lengths, fold_order):
    local_len = queries.shape[1]
    head_width = queries.shape[2]
    half_len = local_len // 2
    scaling = head_width ** (-0.5)
    seq_index = lax.axis_index("seq")
    row_index = lax.axis_index("head") // HEAD_COUNT
    row_count = keys.shape[0]
    span_ids = jnp.arange(fold_order.shape[0], dtype=jnp.int32)
    lengths = lax.dynamic_index_in_dim(doc_lengths, row_index, 0, keepdims=False)
    starts = jnp.cumsum(lengths, dtype=jnp.int32) - lengths

    def locate(indices):
        block_of = indices // half_len
        anchor = jnp.sum(
            jnp.where(block_of[:, None] == span_ids[None, :], fold_order[None, :], 0),
            axis=1,
            dtype=jnp.int32,
        )
        position = anchor * half_len + indices % half_len
        document = jnp.sum(
            (position[:, None] >= starts[None, :]).astype(jnp.int32), axis=1, dtype=jnp.int32
        )
        return (position, document)

    def allowed_pairs(query_place, key_place):
        return (query_place[1][:, None] == key_place[1][None, :]) & (
            key_place[0][None, :] <= query_place[0][:, None]
        )

    local_rows = jnp.arange(local_len, dtype=jnp.int32)
    own_place = locate(seq_index * local_len + local_rows)
    query_rows = queries[0]
    grad_out = d_out[0]
    key_row = lax.dynamic_index_in_dim(keys, row_index, 0, keepdims=False)
    value_row = lax.dynamic_index_in_dim(values, row_index, 0, keepdims=False)
    key_part = lax.all_gather(key_row, "seq", axis=0, tiled=True)
    value_part = lax.all_gather(value_row, "seq", axis=0, tiled=True)
    allowed = allowed_pairs(own_place, locate(jnp.arange(key_part.shape[0], dtype=jnp.int32)))
    run_max = jnp.full((local_len, 1), masked_value, jnp.float32)
    scores = jnp.where(allowed, contract_last(query_rows, key_part) * scaling, masked_value)
    new_max = jnp.maximum(run_max, jnp.max(scores, axis=1, keepdims=True))
    weights = jnp.where(allowed, jnp.exp(scores - new_max), 0.0)
    sum_next = jnp.sum(weights, axis=1, keepdims=True)
    acc_next = jnp.dot(weights.astype(jnp.bfloat16), value_part, preferred_element_type=jnp.float32)
    log_norm = new_max + jnp.log(sum_next)
    output = acc_next / sum_next
    grad_dot = jnp.sum(grad_out.astype(jnp.float32) * output, axis=1, keepdims=True)
    key_part = lax.all_gather(key_row, "seq", axis=0, tiled=True)
    value_part = lax.all_gather(value_row, "seq", axis=0, tiled=True)
    row_total = key_part.shape[0]
    allowed = allowed_pairs(own_place, locate(jnp.arange(row_total, dtype=jnp.int32)))
    part_query, part_key, part_value = block_grads(
        query_rows, grad_out, log_norm, grad_dot, key_part, value_part, allowed, scaling
    )
    full_keys = part_key
    full_values = part_value
    grad_query, full_keys, full_values = (part_query, full_keys, full_values)
    seq_keys, seq_values = (
        lax.psum_scatter(
            full_keys.astype(jnp.bfloat16), "seq", scatter_dimension=0, tiled=True
        ).astype(jnp.float32),
        lax.psum_scatter(
            full_values.astype(jnp.bfloat16), "seq", scatter_dimension=0, tiled=True
        ).astype(jnp.float32),
    )
    grad_keys, grad_values = owner_blocks(seq_keys, seq_values, row_count)
    grad_queries = grad_query.astype(jnp.bfloat16)[None]
    return (grad_queries, grad_keys, grad_values)


MESH = pl.DeviceIdType.MESH


def fused_kernel(
    depths,
    q_hbm,
    k_hbm,
    v_hbm,
    o_hbm,
    len_hbm,
    fold_hbm,
    gq_ref,
    gk_ref,
    gv_ref,
    q_ref,
    o_ref,
    len_ref,
    fold_ref,
    load,
    kv,
    scores,
    probs,
    p_low,
    ds_low,
    own,
    d2d_out,
    d2d_in,
    k1_out,
    k1_in,
    v1_out,
    v1_in,
    k2_out,
    k2_in,
    v2_out,
    v2_in,
    z_out,
    z_in,
    send,
    recv,
    ready,
):
    z_count = depths
    rows, width = k_hbm.shape
    scaling = width ** (-0.5)
    block_total = fold_ref.shape[0]
    doc_total = len_ref.shape[1]
    blocks = block_total // 4
    block_len = rows // blocks
    group = rows // z_count
    piece = group // 2
    part = rows // 4
    bf16 = jnp.bfloat16
    f32 = jnp.float32

    seq = lax.axis_index("seq")
    head = lax.axis_index("head")
    y, c = seq // 2, seq % 2
    z, x = head // 2, head % 2
    partner = {"seq": y * 2 + (1 - c), "head": head}
    y_peer = {"seq": (1 - y) * 2 + c, "head": head}
    x_peer = {"seq": seq, "head": z * 2 + (1 - x)}

    def z_peer(d):
        return {"seq": seq, "head": ((z + d) % z_count) * 2 + x}

    barrier = pltpu.get_barrier_semaphore()
    for peer in (partner, y_peer, x_peer):
        pl.semaphore_signal(barrier, inc=1, device_id=peer, device_id_type=MESH)

    def tell_line(semaphore):
        @pl.when(z > 0)
        def _():
            pl.semaphore_signal(
                semaphore,
                inc=1,
                device_id={"seq": seq, "head": (z - 1) * 2 + x},
                device_id_type=MESH,
            )

        @pl.when(z < z_count - 1)
        def _():
            pl.semaphore_signal(
                semaphore,
                inc=1,
                device_id={"seq": seq, "head": (z + 1) * 2 + x},
                device_id_type=MESH,
            )

    line_peers = (z + z_count - 1) // z_count + (2 * z_count - 2 - z) // z_count
    tell_line(barrier)

    loads = [
        pltpu.make_async_copy(src, dst, load.at[i])
        for i, (src, dst) in enumerate(
            (
                (k_hbm, kv.at[0, 0]),
                (v_hbm, kv.at[0, 1]),
                (fold_hbm, fold_ref),
                (len_hbm, len_ref),
                (q_hbm, q_ref),
                (o_hbm, o_ref),
            )
        )
    ]
    for copy in loads:
        copy.start()

    issued = []

    def remote(src, dst, peer):
        i = len(issued)
        copy = pltpu.make_async_remote_copy(
            src_ref=src,
            dst_ref=dst,
            send_sem=send.at[i],
            recv_sem=recv.at[i],
            device_id=peer,
            device_id_type=MESH,
        )
        copy.start()
        issued.append(copy)
        return copy

    pl.semaphore_wait(barrier, 3 + line_peers)

    z_low = z % 2
    z_pair = {"seq": seq, "head": (z + 1 - 2 * z_low) * 2 + x}

    def quarter(flip_x, flip_z):
        at_x = 1 - x if flip_x else x
        at_z = 1 - z_low if flip_z else z_low
        return pl.ds(pl.multiple_of((at_x * 2 + at_z) * part, part), part)

    y_copies = []
    for i in range(4):
        at = quarter(i // 2, i // 2)
        if i < 2:
            loads[i].wait()
        y_copies.append(remote(kv.at[0, i % 2, at], kv.at[2, i % 2, at], y_peer))
    near = [remote(kv.at[0, i], kv.at[1, i], partner) for i in range(2)]
    tell_line(ready.at[0])
    for copy in loads[2:]:
        copy.wait()

    lane = lax.broadcasted_iota(jnp.int32, (1, rows), 1)
    place = jnp.zeros((1, rows), jnp.int32)
    for b in range(blocks):
        at = fold_ref[seq * blocks + b] * block_len + lane - b * block_len
        place = jnp.where(lane // block_len == b, at, place)
    first = jnp.zeros((1, rows), jnp.int32)
    start = jnp.int32(0)
    for d in range(doc_total):
        first = jnp.where(place >= start, start, first)
        start = start + len_ref[0, d]
    depth = lax.broadcasted_iota(jnp.int32, (block_len, rows), 0)

    def take(slot, state):
        top, total, dot_sum = state
        s_index = ((y + slot // 2) % 2) * 2 + (c + slot) % 2
        for b in range(blocks):
            at = slice(b * block_len, (b + 1) * block_len)
            base = fold_ref[s_index * blocks + b] * block_len
            part_scores = contract_last(kv[slot, 0, at], q_ref[...]) * scaling
            seen = (depth >= first - base) & (depth <= place - base)
            part_scores = jnp.where(seen, part_scores, masked_value)
            scores[slot, at] = part_scores
            part_probs = contract_last(kv[slot, 1, at], o_ref[...])
            probs[slot, at] = part_probs
            new_top = jnp.maximum(top, jnp.max(part_scores, axis=0, keepdims=True))
            weights = jnp.exp(part_scores - new_top)
            fade = jnp.exp(top - new_top)
            total = total * fade + jnp.sum(weights, axis=0, keepdims=True)
            dot_sum = dot_sum * fade + jnp.sum(
                weights * part_probs, axis=0, keepdims=True
            )
            top = new_top
        return (top, total, dot_sum)

    state = (
        jnp.full((1, rows), masked_value, f32),
        jnp.zeros((1, rows), f32),
        jnp.zeros((1, rows), f32),
    )
    state = take(0, state)
    for copy in near:
        copy.wait_recv()
    state = take(1, state)

    for step in range(z_count - 2):
        pl.semaphore_wait(ready.at[step], line_peers)
        if step + 1 < z_count - 2:
            tell_line(ready.at[step + 1])

    x_copies, z_copies, far = [], [], []

    def hand_on(i, at):
        far.append(remote(kv.at[2, i, at], kv.at[3, i, at], partner))

    for i in range(2):
        y_copies[i].wait_recv()
        at = quarter(0, 0)
        block = kv.at[2, i, at]
        x_copies.append(remote(block, block, x_peer))
        z_copies.append(remote(block, block, z_pair))
        hand_on(i, at)
    for i in range(2):
        y_copies[2 + i].wait_recv()
        hand_on(i, quarter(1, 1))
        x_copies[i].wait_recv()
        hand_on(i, quarter(1, 0))
        z_copies[i].wait_recv()
        hand_on(i, quarter(0, 1))
    state = take(2, state)
    for copy in far:
        copy.wait_recv()
    state = take(3, state)
    top, total, dot_sum = state
    log_norm = top + jnp.log(total)
    grad_dot = dot_sum / total

    middle = z_count // 2
    far_first = [middle] + [d for d in range(1, z_count) if d != middle] + [0]

    def group_rows(j):
        return pl.ds(pl.multiple_of(((z + far_first[j]) % z_count) * group, group), group)

    def grads(j):
        at = group_rows(j)
        for slot in range(4):
            to = slice(slot * group, (slot + 1) * group)
            weights = jnp.exp(scores[slot, at] - log_norm)
            p_low[to] = weights.astype(bf16)
            ds_low[j, to] = (weights * (probs[slot, at] - grad_dot)).astype(bf16)
        part_key = (
            jnp.dot(ds_low[j], q_ref[...], preferred_element_type=f32) * scaling
        )
        part_value = jnp.dot(p_low[...], o_ref[...], preferred_element_type=f32)
        for n, item in enumerate((part_key, part_value)):
            for r in range(2):
                own[j, n, r] = item[2 * r * group : (2 * r + 1) * group]
                d2d_out[j, n, r] = item[
                    (2 * r + 1) * group : (2 * r + 2) * group
                ].astype(bf16)
        return remote(d2d_out.at[j], d2d_in.at[j], partner)

    mine = pl.ds(pl.multiple_of(x * piece, piece), piece)
    other = pl.ds(pl.multiple_of((1 - x) * piece, piece), piece)

    def first_hop(j, copy):
        copy.wait_recv()
        own[j] = own[j] + d2d_in[j].astype(f32)
        for r in range(2):
            k1_out[j, r] = own[j, 0, r, other].astype(bf16)
        v1_out[j] = own[j, 1, 1].astype(bf16)
        return (
            remote(k1_out.at[j], k1_in.at[j], x_peer),
            remote(v1_out.at[j], v1_in.at[j], y_peer),
        )

    def second_hop(j, copies):
        copies[0].wait_recv()
        k2_out[j] = (own[j, 0, 1, mine] + k1_in[j, 1].astype(f32)).astype(bf16)
        key_copy = remote(k2_out.at[j], k2_in.at[j], y_peer)
        copies[1].wait_recv()
        v2_out[j] = (own[j, 1, 0, other] + v1_in[j, other].astype(f32)).astype(bf16)
        value_copy = remote(v2_out.at[j], v2_in.at[j], x_peer)
        return (key_copy, value_copy)

    def third_hop(j, copies):
        copies[0].wait_recv()
        key_sum = own[j, 0, 0, mine] + k1_in[j, 0].astype(f32) + k2_in[j].astype(f32)
        copies[1].wait_recv()
        value_sum = (
            own[j, 1, 0, mine] + v1_in[j, mine].astype(f32) + v2_in[j].astype(f32)
        )
        if j == z_count - 1:
            return (key_sum, value_sum)
        z_out[j, 0] = key_sum.astype(bf16)
        z_out[j, 1] = value_sum.astype(bf16)
        return remote(z_out.at[j], z_in.at[j], z_peer(far_first[j]))

    def query_part(j):
        at = group_rows(j)
        out = None
        for slot in range(4):
            to = slice(slot * group, (slot + 1) * group)
            item = contract_first(ds_low[j, to], kv[slot, 0, at])
            out = item if out is None else out + item
        return out

    grad_query = None
    near_sums, hops, later, last = [], [], [], []
    for j in range(z_count):
        near_sums.append(grads(j))
        if j > 0:
            hops.append(first_hop(j - 1, near_sums[j - 1]))
    for j in range(z_count):
        later.append(second_hop(j, hops[j]))
        if j == 0:
            hops.append(first_hop(z_count - 1, near_sums[z_count - 1]))
        item = query_part(j)
        grad_query = item if grad_query is None else grad_query + item
        if j > 0:
            last.append(third_hop(j - 1, later[j - 1]))
    gq_ref[...] = (grad_query * scaling).astype(bf16)
    last.append(third_hop(z_count - 1, later[z_count - 1]))
    key_sum, value_sum = last[-1]
    for j in range(z_count - 1):
        last[j].wait_recv()
        key_sum = key_sum + z_in[j, 0].astype(f32)
        value_sum = value_sum + z_in[j, 1].astype(f32)
    gk_ref[...] = key_sum
    gv_ref[...] = value_sum
    for copy in issued:
        copy.wait_send()


def store_kernel(*refs):
    copies = [
        pltpu.make_async_copy(refs[i], refs[3 + i], refs[6].at[i]) for i in range(3)
    ]
    for copy in copies:
        copy.start()
    for copy in copies:
        copy.wait()


def fused_device(queries, keys, values, d_out, doc_lengths, fold_order):
    z_count = lax.axis_size("head") // 2
    _, rows, width = queries.shape
    group = rows // z_count
    piece = group // 2
    low, full = jnp.bfloat16, jnp.float32
    vmem = pl.BlockSpec(memory_space=pltpu.VMEM)
    copies = 4 + 2 + 4 + 8 + 5 * z_count + z_count - 1
    hbm = pl.BlockSpec(memory_space=pltpu.HBM)
    grad_query, grad_key, grad_value = pl.pallas_call(
        functools.partial(fused_kernel, z_count),
        out_shape=(
            pltpu.VMEM((rows, width), low),
            pltpu.VMEM((piece, width), full),
            pltpu.VMEM((piece, width), full),
        ),
        in_specs=[hbm] * 6,
        out_specs=(vmem,) * 3,
        scratch_shapes=[
            pltpu.VMEM((rows, width), low),
            pltpu.VMEM((rows, width), low),
            pltpu.SMEM(doc_lengths.shape, jnp.int32),
            pltpu.SMEM(fold_order.shape, jnp.int32),
            pltpu.SemaphoreType.DMA((6,)),
            pltpu.VMEM((4, 2, rows, width), low),
            pltpu.VMEM((4, rows, rows), full),
            pltpu.VMEM((4, rows, rows), full),
            pltpu.VMEM((4 * group, rows), low),
            pltpu.VMEM((z_count, 4 * group, rows), low),
            pltpu.VMEM((z_count, 2, 2, group, width), full),
            pltpu.VMEM((z_count, 2, 2, group, width), low),
            pltpu.VMEM((z_count, 2, 2, group, width), low),
            pltpu.VMEM((z_count, 2, piece, width), low),
            pltpu.VMEM((z_count, 2, piece, width), low),
            pltpu.VMEM((z_count, group, width), low),
            pltpu.VMEM((z_count, group, width), low),
            pltpu.VMEM((z_count, piece, width), low),
            pltpu.VMEM((z_count, piece, width), low),
            pltpu.VMEM((z_count, piece, width), low),
            pltpu.VMEM((z_count, piece, width), low),
            pltpu.VMEM((z_count - 1, 2, piece, width), low),
            pltpu.VMEM((z_count - 1, 2, piece, width), low),
            pltpu.SemaphoreType.DMA((copies,)),
            pltpu.SemaphoreType.DMA((copies,)),
            pltpu.SemaphoreType.REGULAR((z_count - 2,)),
        ],
        compiler_params=pltpu.CompilerParams(
            collective_id=0, has_side_effects=True, vmem_limit_bytes=60 * 1024 * 1024
        ),
        name="fused_grads",
    )(
        *(
            pltpu.with_memory_space_constraint(item, pltpu.HBM)
            for item in (
                queries[0], keys[0], values[0], d_out[0], doc_lengths, fold_order
            )
        )
    )
    outs = (grad_query, grad_key, grad_value)
    outs = pl.pallas_call(
        store_kernel,
        out_shape=tuple(jax.ShapeDtypeStruct(item.shape, item.dtype) for item in outs),
        in_specs=[vmem] * 3,
        out_specs=(hbm,) * 3,
        scratch_shapes=[pltpu.SemaphoreType.DMA((3,))],
        compiler_params=pltpu.CompilerParams(vmem_limit_bytes=4 * 1024 * 1024),
        name="store_grads",
    )(*outs)
    return tuple(item[None] for item in outs)


def solution(mesh):
    in_specs = (
        P("head", "seq", None),
        P(None, "seq", None),
        P(None, "seq", None),
        P("head", "seq", None),
        P(),
        P(),
    )
    out_specs = (
        P("head", "seq", None),
        P(None, ("seq", "head"), None),
        P(None, ("seq", "head"), None),
    )
    small = mesh.shape["seq"] == 4 and mesh.shape["head"] == HEAD_COUNT
    return jax.shard_map(
        fused_device if small else per_device,
        mesh=mesh,
        in_specs=in_specs,
        out_specs=out_specs,
        check_vma=False,
    )
```

profile of v0, /device:TPU:0, one launch (start us, length us, event | category | flops | bytes accessed | tf_op | source)
XLA Modules:
  0.0 33.8 jit_solution(3194131650039223428)
XLA Ops:
  0.6 32.4 %fused_grads.1 = (bf16[512,256]{1,0:T(8,128)(2,1)S(1)}, f32[64,256]{1,0:T(8,128)S(1)}, f32[64,256]{1,0:T(8,128)S(1)}) custom-call(bf16[512,256]{1,0:T(8,128)(2,1)} %bitcast.7, bf16[512,256]{1,0:T(8,128)(2,1)} %bitcast.8, bf16[512,256]{1,0:T(8,128)(2,1)} %bitcast.9, bf16[512,256]{1,0:T(8,128)(2,1)} %bitcast.10, s32[1,8]{1,0:T(1,128)} %len_hbm.1, s32[8]{0:T(128)} %fold_hbm.1), custom_call_target="tpu_custom_call" | custom-call | tf_op jit(solution)/shard_map/fused_grads/pallas_call | solution.py:467
  33.0 0.8 %store_grads.1 = (bf16[512,256]{1,0:T(8,128)(2,1)}, f32[64,256]{1,0:T(8,128)}, f32[64,256]{1,0:T(8,128)}) custom-call(bf16[512,256]{1,0:T(8,128)(2,1)S(1)} %get-tuple-element.9.refs_0_, f32[64,256]{1,0:T(8,128)S(1)} %get-tuple-element.10.refs_1_, f32[64,256]{1,0:T(8,128)S(1)} %get-tuple-element.11.refs_2_), custom_call_target="tpu_custom_call" | custom-call | tf_op jit(solution)/shard_map/store_grads/pallas_call | solution.py:517
where the time goes:
time: 33.9 us; the launch traced here: 33.8 us
  Pallas kernels  33.1 us (98%)
  between operations  0.64 us (2%)
    pallas_call x1, Pallas kernels, fused_device(): pl.pallas_call(functools.partial(fused_kernel, z_count), out_shape=(pltpu...  32.4 us
    pallas_call x1, Pallas kernels, fused_device(): pl.pallas_call(store_kernel, out_shape=tuple((jax.ShapeDtypeStruct(item.s...  0.77 us

commit v1 on v0

--- a/solution.py
+++ b/solution.py
@@ -132,7 +132,7 @@
 
 
 def fused_kernel(
-    depths,
+    z_count,
     q_hbm,
     k_hbm,
     v_hbm,
@@ -144,32 +144,34 @@
     gv_ref,
     q_ref,
     o_ref,
+    q_low,
     len_ref,
     fold_ref,
     load,
     kv,
     scores,
     probs,
+    top_at,
     p_low,
     ds_low,
+    k_sorted,
+    stat_out,
+    stat_in,
     own,
-    d2d_out,
-    d2d_in,
-    k1_out,
-    k1_in,
-    v1_out,
-    v1_in,
-    k2_out,
-    k2_in,
-    v2_out,
-    v2_in,
+    first_out,
+    first_in,
+    next_out,
+    next_in,
     z_out,
     z_in,
+    gq_out,
+    gq_in,
     send,
     recv,
+    z_send,
+    z_recv,
     ready,
 ):
-    z_count = depths
     rows, width = k_hbm.shape
     scaling = width ** (-0.5)
     block_total = fold_ref.shape[0]
@@ -190,9 +192,6 @@
     y_peer = {"seq": (1 - y) * 2 + c, "head": head}
     x_peer = {"seq": seq, "head": z * 2 + (1 - x)}
 
-    def z_peer(d):
-        return {"seq": seq, "head": ((z + d) % z_count) * 2 + x}
-
     barrier = pltpu.get_barrier_semaphore()
     for peer in (partner, y_peer, x_peer):
         pl.semaphore_signal(barrier, inc=1, device_id=peer, device_id_type=MESH)
@@ -219,16 +218,18 @@
     line_peers = (z + z_count - 1) // z_count + (2 * z_count - 2 - z) // z_count
     tell_line(barrier)
 
+    near_half = pl.ds(0, rows)
+    far_half = pl.ds(rows, rows)
     loads = [
         pltpu.make_async_copy(src, dst, load.at[i])
         for i, (src, dst) in enumerate(
             (
                 (k_hbm, kv.at[0, 0]),
                 (v_hbm, kv.at[0, 1]),
+                (q_hbm, q_ref.at[near_half]),
+                (o_hbm, o_ref.at[near_half]),
                 (fold_hbm, fold_ref),
                 (len_hbm, len_ref),
-                (q_hbm, q_ref),
-                (o_hbm, o_ref),
             )
         )
     ]
@@ -251,6 +252,16 @@
         issued.append(copy)
         return copy
 
+    def is_at(at):
+        return 1 // (1 + (z - at) * (z - at))
+
+    tables = [
+        sorted(range(z_count), key=lambda to: (-abs(to - at), to)) for at in range(z_count)
+    ]
+    farthest = [
+        sum(tables[at][j] * is_at(at) for at in range(z_count)) for j in range(z_count)
+    ]
+
     pl.semaphore_wait(barrier, 3 + line_peers)
 
     z_low = z % 2
@@ -259,189 +270,253 @@
     def quarter(flip_x, flip_z):
         at_x = 1 - x if flip_x else x
         at_z = 1 - z_low if flip_z else z_low
-        return pl.ds(pl.multiple_of((at_x * 2 + at_z) * part, part), part)
+        return pl.multiple_of((at_x * 2 + at_z) * part, part)
 
     y_copies = []
     for i in range(4):
-        at = quarter(i // 2, i // 2)
+        at = pl.ds(quarter(i // 2, i // 2), part)
         if i < 2:
             loads[i].wait()
-        y_copies.append(remote(kv.at[0, i % 2, at], kv.at[2, i % 2, at], y_peer))
-    near = [remote(kv.at[0, i], kv.at[1, i], partner) for i in range(2)]
+        y_copies.append(remote(kv.at[0, i % 2, at], kv.at[1, i % 2, at], y_peer))
+    loads[2].wait()
+    q_copy = remote(q_ref.at[near_half], q_ref.at[far_half], partner)
+    loads[3].wait()
+    o_copy = remote(o_ref.at[near_half], o_ref.at[far_half], partner)
     tell_line(ready.at[0])
-    for copy in loads[2:]:
+    for copy in loads[4:]:
         copy.wait()
 
-    lane = lax.broadcasted_iota(jnp.int32, (1, rows), 1)
-    place = jnp.zeros((1, rows), jnp.int32)
-    for b in range(blocks):
-        at = fold_ref[seq * blocks + b] * block_len + lane - b * block_len
+    lane = lax.broadcasted_iota(jnp.int32, (1, 2 * rows), 1)
+    place = jnp.zeros((1, 2 * rows), jnp.int32)
+    mate = y * 2 + (1 - c)
+    for b in range(2 * blocks):
+        index = seq * blocks + b if b < blocks else mate * blocks + b - blocks
+        at = fold_ref[index] * block_len + lane - b * block_len
         place = jnp.where(lane // block_len == b, at, place)
-    first = jnp.zeros((1, rows), jnp.int32)
+    first = jnp.zeros((1, 2 * rows), jnp.int32)
     start = jnp.int32(0)
     for d in range(doc_total):
         first = jnp.where(place >= start, start, first)
         start = start + len_ref[0, d]
-    depth = lax.broadcasted_iota(jnp.int32, (block_len, rows), 0)
-
-    def take(slot, state):
-        top, total, dot_sum = state
-        s_index = ((y + slot // 2) % 2) * 2 + (c + slot) % 2
-        for b in range(blocks):
-            at = slice(b * block_len, (b + 1) * block_len)
-            base = fold_ref[s_index * blocks + b] * block_len
-            part_scores = contract_last(kv[slot, 0, at], q_ref[...]) * scaling
-            seen = (depth >= first - base) & (depth <= place - base)
-            part_scores = jnp.where(seen, part_scores, masked_value)
-            scores[slot, at] = part_scores
-            part_probs = contract_last(kv[slot, 1, at], o_ref[...])
-            probs[slot, at] = part_probs
-            new_top = jnp.maximum(top, jnp.max(part_scores, axis=0, keepdims=True))
-            weights = jnp.exp(part_scores - new_top)
-            fade = jnp.exp(top - new_top)
-            total = total * fade + jnp.sum(weights, axis=0, keepdims=True)
-            dot_sum = dot_sum * fade + jnp.sum(
-                weights * part_probs, axis=0, keepdims=True
-            )
-            top = new_top
-        return (top, total, dot_sum)
-
-    state = (
-        jnp.full((1, rows), masked_value, f32),
-        jnp.zeros((1, rows), f32),
-        jnp.zeros((1, rows), f32),
-    )
-    state = take(0, state)
-    for copy in near:
-        copy.wait_recv()
-    state = take(1, state)
-
-    for step in range(z_count - 2):
+
+    tops, sums, dots = [[], []], [[], []], [[], []]
+
+    def take_keys(slot, off, count, half):
+        shard = seq if slot == 0 else (1 - y) * 2 + c
+        cols = slice(half * rows, (half + 1) * rows)
+        at = pl.ds(off, count)
+        base = fold_ref[shard * blocks + off // block_len] * block_len + off % block_len
+        depth = lax.broadcasted_iota(jnp.int32, (count, rows), 0)
+        item = contract_last(kv[slot, 0, at], q_low[cols])
+        seen = (depth >= first[:, cols] - base) & (depth <= place[:, cols] - base)
+        item = jnp.where(seen, item, masked_value)
+        top = jnp.max(item, axis=0, keepdims=True)
+        item = jnp.exp(item - top)
+        scores[slot, at, cols] = item
+        for b in range(count // part):
+            top_at[slot, off // part + b, :, cols] = top
+        tops[half].append(top)
+        sums[half].append(jnp.sum(item, axis=0, keepdims=True))
+
+    def take_values(slot, off, count, half):
+        cols = slice(half * rows, (half + 1) * rows)
+        at = pl.ds(off, count)
+        item = contract_last(kv[slot, 1, at], o_ref[cols])
+        probs[slot, at, cols] = item
+        dots[half].append(jnp.sum(scores[slot, at, cols] * item, axis=0, keepdims=True))
+
+    def line_step(step):
         pl.semaphore_wait(ready.at[step], line_peers)
         if step + 1 < z_count - 2:
             tell_line(ready.at[step + 1])
 
-    x_copies, z_copies, far = [], [], []
-
-    def hand_on(i, at):
-        far.append(remote(kv.at[2, i, at], kv.at[3, i, at], partner))
-
-    for i in range(2):
+    q_low[0:rows] = (q_ref[0:rows].astype(f32) * scaling).astype(bf16)
+    for b in range(blocks):
+        take_keys(0, b * block_len, block_len, 0)
+        take_values(0, b * block_len, block_len, 0)
+
+    line_step(0)
+    q_copy.wait_recv()
+    q_low[rows : 2 * rows] = (q_ref[rows : 2 * rows].astype(f32) * scaling).astype(bf16)
+    for b in range(blocks):
+        take_keys(0, b * block_len, block_len, 1)
+
+    x_copies, z_copies = [], []
+
+    def relay(i):
         y_copies[i].wait_recv()
-        at = quarter(0, 0)
-        block = kv.at[2, i, at]
+        block = kv.at[1, i, pl.ds(quarter(0, 0), part)]
         x_copies.append(remote(block, block, x_peer))
         z_copies.append(remote(block, block, z_pair))
-        hand_on(i, at)
-    for i in range(2):
-        y_copies[2 + i].wait_recv()
-        hand_on(i, quarter(1, 1))
-        x_copies[i].wait_recv()
-        hand_on(i, quarter(1, 0))
-        z_copies[i].wait_recv()
-        hand_on(i, quarter(0, 1))
-    state = take(2, state)
-    for copy in far:
+
+    def take_far(take, flip_x, flip_z):
+        for half in range(2):
+            take(1, quarter(flip_x, flip_z), part, half)
+
+    relay(0)
+    o_copy.wait_recv()
+    for b in range(blocks):
+        take_values(0, b * block_len, block_len, 1)
+    take_far(take_keys, 0, 0)
+    relay(1)
+    take_far(take_values, 0, 0)
+    y_copies[2].wait_recv()
+    take_far(take_keys, 1, 1)
+    z_copies[0].wait_recv()
+    take_far(take_keys, 0, 1)
+    x_copies[0].wait_recv()
+    take_far(take_keys, 1, 0)
+
+    def swapped(i):
+        return jnp.concatenate(
+            [stat_in[i, :, rows : 2 * rows], stat_in[i, :, 0:rows]], axis=1
+        )
+
+    log_sums = []
+    for half in range(2):
+        top = functools.reduce(jnp.maximum, tops[half])
+        total = sum(s * jnp.exp(t - top) for s, t in zip(sums[half], tops[half]))
+        log_sums.append(top + jnp.log(total))
+        stat_out[0, :, half * rows : (half + 1) * rows] = log_sums[half]
+    norm_copy = remote(stat_out.at[0], stat_in.at[0], partner)
+    for step in range(1, z_count - 2):
+        line_step(step)
+
+    y_copies[3].wait_recv()
+    take_far(take_values, 1, 1)
+    z_copies[1].wait_recv()
+    take_far(take_values, 0, 1)
+    x_copies[1].wait_recv()
+    take_far(take_values, 1, 0)
+
+    for half in range(2):
+        stat_out[1, :, half * rows : (half + 1) * rows] = sum(
+            d * jnp.exp(t - log_sums[half]) for d, t in zip(dots[half], tops[half])
+        )
+    dot_copy = remote(stat_out.at[1], stat_in.at[1], partner)
+
+    def pieces(j):
+        mine = pl.ds(pl.multiple_of(farthest[j] * group + x * piece, piece), piece)
+        other = pl.ds(pl.multiple_of(farthest[j] * group + (1 - x) * piece, piece), piece)
+        return [(0, mine), (0, other), (1, mine), (1, other)]
+
+    def first_hop(u, item, x_first):
+        near_mine, near_other, far_mine, far_other = (
+            item[i * piece : (i + 1) * piece] for i in range(4)
+        )
+        kept, sent = (far_mine, near_other) if x_first else (near_other, far_mine)
+        own[u, 0:piece] = near_mine
+        own[u, piece:group] = kept
+        first_out[u, 0:piece] = sent.astype(bf16)
+        first_out[u, piece:group] = far_other.astype(bf16)
+        peers = (x_peer, y_peer) if x_first else (y_peer, x_peer)
+        return (remote(first_out.at[u], first_in.at[u], peers[0]), peers[1])
+
+    def second_hop(u, hop):
+        hop[0].wait_recv()
+        next_out[u] = (own[u, piece:group] + first_in[u, piece:group].astype(f32)).astype(bf16)
+        return remote(next_out.at[u], next_in.at[u], hop[1])
+
+    z_copies_out = []
+
+    def z_copy(n, j, d):
+        return pltpu.make_async_remote_copy(
+            src_ref=z_out.at[n, j],
+            dst_ref=z_in.at[n, d],
+            send_sem=z_send.at[n, j],
+            recv_sem=z_recv.at[n, d],
+            device_id={"seq": seq, "head": ((z + d + 1) % z_count) * 2 + x},
+            device_id_type=MESH,
+        )
+
+    def third_hop(u, copy):
+        n, j = u // z_count, u % z_count
         copy.wait_recv()
-    state = take(3, state)
-    top, total, dot_sum = state
-    log_norm = top + jnp.log(total)
-    grad_dot = dot_sum / total
-
-    middle = z_count // 2
-    far_first = [middle] + [d for d in range(1, z_count) if d != middle] + [0]
-
-    def group_rows(j):
-        return pl.ds(pl.multiple_of(((z + far_first[j]) % z_count) * group, group), group)
-
-    def grads(j):
-        at = group_rows(j)
-        for slot in range(4):
-            to = slice(slot * group, (slot + 1) * group)
-            weights = jnp.exp(scores[slot, at] - log_norm)
-            p_low[to] = weights.astype(bf16)
-            ds_low[j, to] = (weights * (probs[slot, at] - grad_dot)).astype(bf16)
-        part_key = (
-            jnp.dot(ds_low[j], q_ref[...], preferred_element_type=f32) * scaling
-        )
-        part_value = jnp.dot(p_low[...], o_ref[...], preferred_element_type=f32)
-        for n, item in enumerate((part_key, part_value)):
-            for r in range(2):
-                own[j, n, r] = item[2 * r * group : (2 * r + 1) * group]
-                d2d_out[j, n, r] = item[
-                    (2 * r + 1) * group : (2 * r + 2) * group
-                ].astype(bf16)
-        return remote(d2d_out.at[j], d2d_in.at[j], partner)
-
-    mine = pl.ds(pl.multiple_of(x * piece, piece), piece)
-    other = pl.ds(pl.multiple_of((1 - x) * piece, piece), piece)
-
-    def first_hop(j, copy):
-        copy.wait_recv()
-        own[j] = own[j] + d2d_in[j].astype(f32)
-        for r in range(2):
-            k1_out[j, r] = own[j, 0, r, other].astype(bf16)
-        v1_out[j] = own[j, 1, 1].astype(bf16)
-        return (
-            remote(k1_out.at[j], k1_in.at[j], x_peer),
-            remote(v1_out.at[j], v1_in.at[j], y_peer),
-        )
-
-    def second_hop(j, copies):
-        copies[0].wait_recv()
-        k2_out[j] = (own[j, 0, 1, mine] + k1_in[j, 1].astype(f32)).astype(bf16)
-        key_copy = remote(k2_out.at[j], k2_in.at[j], y_peer)
-        copies[1].wait_recv()
-        v2_out[j] = (own[j, 1, 0, other] + v1_in[j, other].astype(f32)).astype(bf16)
-        value_copy = remote(v2_out.at[j], v2_in.at[j], x_peer)
-        return (key_copy, value_copy)
-
-    def third_hop(j, copies):
-        copies[0].wait_recv()
-        key_sum = own[j, 0, 0, mine] + k1_in[j, 0].astype(f32) + k2_in[j].astype(f32)
-        copies[1].wait_recv()
-        value_sum = (
-            own[j, 1, 0, mine] + v1_in[j, mine].astype(f32) + v2_in[j].astype(f32)
-        )
+        item = own[u, 0:piece] + first_in[u, 0:piece].astype(f32) + next_in[u].astype(f32)
         if j == z_count - 1:
-            return (key_sum, value_sum)
-        z_out[j, 0] = key_sum.astype(bf16)
-        z_out[j, 1] = value_sum.astype(bf16)
-        return remote(z_out.at[j], z_in.at[j], z_peer(far_first[j]))
-
-    def query_part(j):
-        at = group_rows(j)
-        out = None
-        for slot in range(4):
-            to = slice(slot * group, (slot + 1) * group)
-            item = contract_first(ds_low[j, to], kv[slot, 0, at])
-            out = item if out is None else out + item
-        return out
-
-    grad_query = None
-    near_sums, hops, later, last = [], [], [], []
+            return item
+        z_out[n, j] = item.astype(bf16)
+        move = z_copy(n, j, (farthest[j] - z + z_count - 1) % z_count)
+        move.start()
+        z_copies_out.append(move)
+        return None
+
     for j in range(z_count):
-        near_sums.append(grads(j))
-        if j > 0:
-            hops.append(first_hop(j - 1, near_sums[j - 1]))
-    for j in range(z_count):
-        later.append(second_hop(j, hops[j]))
-        if j == 0:
-            hops.append(first_hop(z_count - 1, near_sums[z_count - 1]))
-        item = query_part(j)
-        grad_query = item if grad_query is None else grad_query + item
-        if j > 0:
-            last.append(third_hop(j - 1, later[j - 1]))
-    gq_ref[...] = (grad_query * scaling).astype(bf16)
-    last.append(third_hop(z_count - 1, later[z_count - 1]))
-    key_sum, value_sum = last[-1]
+        for i, (slot, at) in enumerate(pieces(j)):
+            k_sorted[j * 2 * group + i * piece : j * 2 * group + (i + 1) * piece] = kv[slot, 0, at]
+
+    norm_copy.wait_recv()
+    mine, theirs = stat_out[0], swapped(0)
+    top = jnp.maximum(mine, theirs)
+    log_norm = top + jnp.log(jnp.exp(mine - top) + jnp.exp(theirs - top))
+    for slot in range(2):
+        for b in range(4):
+            top_at[slot, b] = jnp.exp(top_at[slot, b] - log_norm)
+
+    hops = {}
+
+    def value_part(j):
+        for i, (slot, at) in enumerate(pieces(j)):
+            weights = scores[slot, at] * top_at[slot, farthest[j]]
+            scores[slot, at] = weights
+            p_low[j, i * piece : (i + 1) * piece] = weights.astype(bf16)
+        item = jnp.dot(p_low[j], o_ref[...], preferred_element_type=f32)
+        hops[j] = first_hop(j, item, j % 2 == 0)
+
     for j in range(z_count - 1):
-        last[j].wait_recv()
-        key_sum = key_sum + z_in[j, 0].astype(f32)
-        value_sum = value_sum + z_in[j, 1].astype(f32)
+        value_part(j)
+    dot_copy.wait_recv()
+    grad_dot = stat_out[1] * jnp.exp(mine - log_norm) + swapped(1) * jnp.exp(theirs - log_norm)
+
+    def key_part(j):
+        for i, (slot, at) in enumerate(pieces(j)):
+            low = (scores[slot, at] * (probs[slot, at] - grad_dot)).astype(bf16)
+            ds_low[j * 2 * group + i * piece : j * 2 * group + (i + 1) * piece] = low
+        at = slice(j * 2 * group, (j + 1) * 2 * group)
+        item = jnp.dot(ds_low[at], q_low[...], preferred_element_type=f32)
+        hops[z_count + j] = first_hop(z_count + j, item, j % 2 == 1)
+
+    def query_part(half):
+        cols = slice(half * rows, (half + 1) * rows)
+        return contract_first(ds_low[:, cols], k_sorted[...])
+
+    later = {}
+
+    def onward(u):
+        later[u] = second_hop(u, hops[u])
+
+    last = z_count - 1
+    key_part(0)
+    key_part(1)
+    onward(0)
+    key_part(2)
+    onward(1)
+    onward(2)
+    value_part(last)
+    key_part(last)
+    for j in range(last):
+        onward(z_count + j)
+        third_hop(j, later[j])
+    gq_out[...] = (query_part(1) * scaling).astype(bf16)
+    gq_copy = remote(gq_out, gq_in, partner)
+    for j in range(last):
+        third_hop(z_count + j, later[z_count + j])
+    onward(last)
+    onward(z_count + last)
+    grad_query = query_part(0)
+    gq_copy.wait_recv()
+    gq_ref[...] = (grad_query * scaling + gq_in[...].astype(f32)).astype(bf16)
+    value_sum = third_hop(last, later[last])
+    for d in range(last):
+        z_copy(0, 0, d).wait_recv()
+        value_sum = value_sum + z_in[0, d].astype(f32)
+    gv_ref[...] = value_sum
+    key_sum = third_hop(z_count + last, later[z_count + last])
+    for d in range(last):
+        z_copy(1, 0, d).wait_recv()
+        key_sum = key_sum + z_in[1, d].astype(f32)
     gk_ref[...] = key_sum
-    gv_ref[...] = value_sum
-    for copy in issued:
+    for copy in issued + z_copies_out:
         copy.wait_send()
 
 
@@ -460,9 +535,10 @@
     _, rows, width = queries.shape
     group = rows // z_count
     piece = group // 2
+    units = 2 * z_count
     low, full = jnp.bfloat16, jnp.float32
     vmem = pl.BlockSpec(memory_space=pltpu.VMEM)
-    copies = 4 + 2 + 4 + 8 + 5 * z_count + z_count - 1
+    copies = 4 + 2 + 4 + 2 + 2 * units + 1
     hbm = pl.BlockSpec(memory_space=pltpu.HBM)
     grad_query, grad_key, grad_value = pl.pallas_call(
         functools.partial(fused_kernel, z_count),
@@ -474,31 +550,34 @@
         in_specs=[hbm] * 6,
         out_specs=(vmem,) * 3,
         scratch_shapes=[
-            pltpu.VMEM((rows, width), low),
-            pltpu.VMEM((rows, width), low),
+            pltpu.VMEM((2 * rows, width), low),
+            pltpu.VMEM((2 * rows, width), low),
+            pltpu.VMEM((2 * rows, width), low),
             pltpu.SMEM(doc_lengths.shape, jnp.int32),
             pltpu.SMEM(fold_order.shape, jnp.int32),
             pltpu.SemaphoreType.DMA((6,)),
-            pltpu.VMEM((4, 2, rows, width), low),
-            pltpu.VMEM((4, rows, rows), full),
-            pltpu.VMEM((4, rows, rows), full),
-            pltpu.VMEM((4 * group, rows), low),
-            pltpu.VMEM((z_count, 4 * group, rows), low),
-            pltpu.VMEM((z_count, 2, 2, group, width), full),
-            pltpu.VMEM((z_count, 2, 2, group, width), low),
-            pltpu.VMEM((z_count, 2, 2, group, width), low),
-            pltpu.VMEM((z_count, 2, piece, width), low),
-            pltpu.VMEM((z_count, 2, piece, width), low),
-            pltpu.VMEM((z_count, group, width), low),
-            pltpu.VMEM((z_count, group, width), low),
-            pltpu.VMEM((z_count, piece, width), low),
-            pltpu.VMEM((z_count, piece, width), low),
-            pltpu.VMEM((z_count, piece, width), low),
-            pltpu.VMEM((z_count, piece, width), low),
-            pltpu.VMEM((z_count - 1, 2, piece, width), low),
-            pltpu.VMEM((z_count - 1, 2, piece, width), low),
+            pltpu.VMEM((2, 2, rows, width), low),
+            pltpu.VMEM((2, rows, 2 * rows), full),
+            pltpu.VMEM((2, rows, 2 * rows), full),
+            pltpu.VMEM((2, 4, 1, 2 * rows), full),
+            pltpu.VMEM((z_count, 2 * group, 2 * rows), low),
+            pltpu.VMEM((2 * rows, 2 * rows), low),
+            pltpu.VMEM((2 * rows, width), low),
+            pltpu.VMEM((2, 1, 2 * rows), full),
+            pltpu.VMEM((2, 1, 2 * rows), full),
+            pltpu.VMEM((units, group, width), full),
+            pltpu.VMEM((units, group, width), low),
+            pltpu.VMEM((units, group, width), low),
+            pltpu.VMEM((units, piece, width), low),
+            pltpu.VMEM((units, piece, width), low),
+            pltpu.VMEM((2, z_count - 1, piece, width), low),
+            pltpu.VMEM((2, z_count - 1, piece, width), low),
+            pltpu.VMEM((rows, width), low),
+            pltpu.VMEM((rows, width), low),
             pltpu.SemaphoreType.DMA((copies,)),
             pltpu.SemaphoreType.DMA((copies,)),
+            pltpu.SemaphoreType.DMA((2, z_count - 1)),
+            pltpu.SemaphoreType.DMA((2, z_count - 1)),
             pltpu.SemaphoreType.REGULAR((z_count - 2,)),
         ],
         compiler_params=pltpu.CompilerParams(

time: 33.9 us -> 31.3 us (0.923)
  Pallas kernels: 33.1 us -> 30.5 us
    pallas_call x1, Pallas kernels: 32.4 us -> 29.7 us  [fused_device(): pl.pallas_call(functools.partial(fused_kernel, z_count), out_shape=(pltpu...]
where the time goes in v1:
time: 31.3 us; the launch traced here: 31.1 us
  Pallas kernels  30.5 us (97%)
  between operations  0.64 us (2%)
    pallas_call x1, Pallas kernels, fused_device(): pl.pallas_call(functools.partial(fused_kernel, z_count), out_shape=(pltpu...  29.7 us
    pallas_call x1, Pallas kernels, fused_device(): pl.pallas_call(store_kernel, out_shape=tuple((jax.ShapeDtypeStruct(item.s...  0.77 us

profile of v1, /device:TPU:0, one launch (start us, length us, event | category | flops | bytes accessed | tf_op | source)
XLA Modules:
  0.0 31.1 jit_solution(15766346226238826006)
XLA Ops:
  0.6 29.7 %fused_grads.1 = (bf16[512,256]{1,0:T(8,128)(2,1)S(1)}, f32[64,256]{1,0:T(8,128)S(1)}, f32[64,256]{1,0:T(8,128)S(1)}) custom-call(bf16[512,256]{1,0:T(8,128)(2,1)} %bitcast.7, bf16[512,256]{1,0:T(8,128)(2,1)} %bitcast.8, bf16[512,256]{1,0:T(8,128)(2,1)} %bitcast.9, bf16[512,256]{1,0:T(8,128)(2,1)} %bitcast.10, s32[1,8]{1,0:T(1,128)} %len_hbm.1, s32[8]{0:T(128)} %fold_hbm.1), custom_call_target="tpu_custom_call" | custom-call | tf_op jit(solution)/shard_map/fused_grads/pallas_call | solution.py:543
  30.4 0.8 %store_grads.1 = (bf16[512,256]{1,0:T(8,128)(2,1)}, f32[64,256]{1,0:T(8,128)}, f32[64,256]{1,0:T(8,128)}) custom-call(bf16[512,256]{1,0:T(8,128)(2,1)S(1)} %get-tuple-element.9.refs_0_, f32[64,256]{1,0:T(8,128)S(1)} %get-tuple-element.10.refs_1_, f32[64,256]{1,0:T(8,128)S(1)} %get-tuple-element.11.refs_2_), custom_call_target="tpu_custom_call" | custom-call | tf_op jit(solution)/shard_map/store_grads/pallas_call | solution.py:596
